TPU v7x, 32 devices: a whole 2x2x4 slice. The times are simulated.
32 devices in a mesh: lon: 8 (over y, x, core), lat: 4 (over z).
Axes of the slice: x: 2, y: 2, z: 4, core: 2. Of those that a mesh axis runs over, the one named last changes fastest.
Arguments:
- surface_forcing: float32 [96, 1024], P('lat', 'lon'), may hold values from -33 to 33
- sea_mask: int32 [96, 1024], P('lat', 'lon'), may hold values 0 or 1
- level_count: int32 [96, 1024], P('lat', 'lon'), may hold values from 1 to 40
- state: float32 [4, 40, 96, 1024], P(None, None, 'lat', 'lon'), may hold values from -6 to 6
Outputs:
- surface_height: float32 [96, 1024], P('lat', 'lon')
- residual: float32 [96, 1024], P('lat', 'lon')
- tendency: float32 [4, 40, 96, 1024], P(None, None, 'lat', 'lon')
All inputs are finite; a program needn't handle non-finite values. No bound on the sum of `sea_mask` on one device may be relied on, other than what follows from the above.
Results may differ from a plain program's by a relative error of at most 0.0003.
Values sent between devices are 32-bit elements; how exact they have to be, the bound alone decides.
A program may use at most 64 MiB of HBM per device.

v0:
```python
import jax
import jax.numpy as jnp
from jax import lax
from jax.sharding import PartitionSpec as P

LEV = 40
ITERS = 4


damping = 0.05
face_scale = 1.0
viscosity = 0.02


def with_halo(cells, sides, width):
    for axis, dim in sides:
        count = lax.axis_size(axis)
        head = lax.slice_in_dim(cells, 0, width, axis=dim)
        tail = lax.slice_in_dim(cells, cells.shape[dim] - width, cells.shape[dim], axis=dim)
        cells = jnp.concatenate(
            [
                lax.ppermute(tail, axis, [(i, (i + 1) % count) for i in range(count)]),
                cells,
                lax.ppermute(head, axis, [((i + 1) % count, i) for i in range(count)]),
            ],
            axis=dim,
        )
    return cells


def trim_rims(field, margin):
    return field[..., margin : field.shape[-2] - margin, margin : field.shape[-1] - margin]


def face_coeffs(depth, width_out, width_in):
    offset = width_in - width_out
    height = depth.shape[0] - 2 * offset
    breadth = depth.shape[1] - 2 * offset
    center = depth[offset : offset + height, offset : offset + breadth]
    east_face = face_scale * jnp.minimum(
        center, depth[offset : offset + height, offset + 1 : offset + 1 + breadth]
    )
    west_face = face_scale * jnp.minimum(
        center, depth[offset : offset + height, offset - 1 : offset - 1 + breadth]
    )
    north_face = face_scale * jnp.minimum(
        center, depth[offset + 1 : offset + 1 + height, offset : offset + breadth]
    )
    south_face = face_scale * jnp.minimum(
        center, depth[offset - 1 : offset - 1 + height, offset : offset + breadth]
    )
    diagonal = damping + east_face + west_face + north_face + south_face
    return (diagonal, east_face, west_face, north_face, south_face)


def operator_apply(padded, coeffs):
    diagonal, east_face, west_face, north_face, south_face = coeffs
    return (
        diagonal * padded[1:-1, 1:-1]
        - east_face * padded[1:-1, 2:]
        - west_face * padded[1:-1, :-2]
        - north_face * padded[2:, 1:-1]
        - south_face * padded[:-2, 1:-1]
    )


def laplace(field, active):
    center = field[..., 1:-1, 1:-1]
    active_center = active[..., 1:-1, 1:-1]
    east_part = active_center * active[..., 1:-1, 2:] * (field[..., 1:-1, 2:] - center)
    west_part = active_center * active[..., 1:-1, :-2] * (center - field[..., 1:-1, :-2])
    north_part = active_center * active[..., 2:, 1:-1] * (field[..., 2:, 1:-1] - center)
    south_part = active_center * active[..., :-2, 1:-1] * (center - field[..., :-2, 1:-1])
    return east_part - west_part + north_part - south_part


def advect(field, active):
    east_flow = field[2]
    north_flow = field[3]
    center = field[..., 1:-1, 1:-1]
    active_center = active[..., 1:-1, 1:-1]
    flow_center = east_flow[..., 1:-1, 1:-1]
    lift_center = north_flow[..., 1:-1, 1:-1]
    east_speed = (
        0.25 * active_center * active[..., 1:-1, 2:] * (flow_center + east_flow[..., 1:-1, 2:])
    )
    west_speed = (
        0.25 * active_center * active[..., 1:-1, :-2] * (flow_center + east_flow[..., 1:-1, :-2])
    )
    north_speed = (
        0.25 * active_center * active[..., 2:, 1:-1] * (lift_center + north_flow[..., 2:, 1:-1])
    )
    south_speed = (
        0.25 * active_center * active[..., :-2, 1:-1] * (lift_center + north_flow[..., :-2, 1:-1])
    )
    return (
        east_speed * (center + field[..., 1:-1, 2:])
        - west_speed * (center + field[..., 1:-1, :-2])
        + north_speed * (center + field[..., 2:, 1:-1])
        - south_speed * (center + field[..., :-2, 1:-1])
    )


def tendency_of(state_wide, active_wide):
    inner_active = trim_rims(active_wide, 1)
    smoothed = laplace(laplace(state_wide, active_wide), inner_active)
    flux = advect(trim_rims(state_wide, 1), inner_active)
    return trim_rims(active_wide, 2) * (-flux - viscosity * smoothed)


def apply_operator(field, coeff_list):
    padded = with_halo(field, (("lon", 1), ("lat", 0)), 1)
    return (operator_apply(padded, coeff_list[0]), 0)


def paired_totals(residual, search, image, width):
    return lax.psum(
        (jnp.sum(trim_rims(residual * search, width)), jnp.sum(trim_rims(image * search, width))),
        ("lon", "lat"),
    )


def paired_solve(forcing, width, coeff_list):
    residual = forcing
    search = residual / coeff_list[width][0]
    image, narrow = apply_operator(search, coeff_list)
    residual = trim_rims(residual, width - narrow)
    search = trim_rims(search, width - narrow)
    width = narrow
    product, curvature = paired_totals(residual, search, image, width)
    alpha_step = product / curvature
    direction = search
    along = image
    solution = jnp.zeros_like(residual)
    for step_index in range(ITERS):
        solution = solution + alpha_step * direction
        residual = residual - alpha_step * along
        if step_index + 1 < ITERS:
            search = residual / coeff_list[width][0]
            image, narrow = apply_operator(search, coeff_list)
            margin = width - narrow
            residual = trim_rims(residual, margin)
            search = trim_rims(search, margin)
            solution = trim_rims(solution, margin)
            direction = trim_rims(direction, margin)
            along = trim_rims(along, margin)
            width = narrow
            product_next, curvature = paired_totals(residual, search, image, width)
            beta_step = product_next / product
            alpha_step = product_next / (curvature - beta_step * product_next / alpha_step)
            product = product_next
            direction = search + beta_step * direction
            along = image + beta_step * along
    return (solution, residual)


def per_device(surface_forcing, sea_mask, level_count, state):
    height = surface_forcing.shape[0]
    rim_width = 2
    columns = jnp.stack([sea_mask, level_count])
    columns_wide = with_halo(columns, (("lon", 2), ("lat", 1)), rim_width)
    rows_global = (
        lax.axis_index("lat") * height
        + jnp.arange(height + 2 * rim_width, dtype=jnp.int32)
        - rim_width
    )
    inside = ((rows_global >= 0) & (rows_global < height * lax.axis_size("lat"))).astype(
        jnp.float32
    )
    sea_wide = columns_wide[0].astype(jnp.float32) * inside[:, None]
    depth = sea_wide * columns_wide[1].astype(jnp.float32) / LEV
    coeff_list = [face_coeffs(depth, width, rim_width) for width in range(rim_width)]
    forcing = trim_rims(sea_wide, rim_width) * surface_forcing
    start_width = 0
    solution, residual = paired_solve(forcing, start_width, coeff_list)
    level_index = jnp.arange(state.shape[1], dtype=jnp.int32)[:, None, None]
    sea_near = trim_rims(sea_wide, rim_width - 2)
    count_near = trim_rims(columns_wide[1], rim_width - 2)
    active_wide = (level_index < count_near[None]).astype(jnp.float32) * sea_near[None]
    state_wide = with_halo(state, (("lon", 3), ("lat", 2)), 2)
    tendency = tendency_of(state_wide, active_wide)
    return (solution, residual, tendency)


def solution(mesh):
    return jax.shard_map(
        per_device,
        mesh=mesh,
        in_specs=(P("lat", "lon"), P("lat", "lon"), P("lat", "lon"), P(None, None, "lat", "lon")),
        out_specs=(P("lat", "lon"), P("lat", "lon"), P(None, None, "lat", "lon")),
        check_vma=False,
    )
```

profile of v0, /device:TPU:0, one launch (start us, length us, event | category | flops | bytes accessed | tf_op | source)
XLA Modules:
  0.0 297.8 jit_solution(5323145204198029798)
XLA Ops:
  0.6 0.9 slice_add_fusion.4
  2.0 2.9 collective-permute-start.1
  4.9 4.1 %fusion.74 = (f32[4,40,24,2]{3,2,1,0:T(8,128)S(1)}, f32[4,40,24,2]{3,2,1,0:T(8,128)}) fusion(f32[4,40,24,128]{3,2,1,0:T(8,128)} %param.7), kind=kLoop, calls=%fused_computation.183 | loop fusion | bytes 122880 | tf_op jit(solution)/shard_map/slice | solution.py:19
  9.0 2.3 copy.22
  11.3 0.7 collective-permute-start.21
  12.0 1.4 copy.21
  13.5 2.2 collective-permute-start.2
  15.7 2.1 collective-permute-start.3
  17.8 1.9 copy.10
  20.1 2.6 collective-permute-start.4
  22.7 1.4 collective-permute-done.5
  24.2 3.5 %collective-permute-start.6 = (f32[1,130]{1,0:T(1,128)S(1)}, f32[1,130]{1,0:T(1,128)S(1)}, u32[]{:S(2)}, u32[]{:S(2)}) collective-permute-start(f32[1,130]{1,0:T(1,128)S(1)} %get-tuple-element.69), channel_id=1, source_target_pairs={{1,0},{2,1},{3,2},{0,3},{5,4},{6,5},{7,6},{4,7},{9,8},{10,9},{11,1... | collective-permute-start | bytes 1568 | tf_op jit(solution)/shard_map/ppermute | solution.py:24
  27.7 1.2 collective-permute-done.6
  28.9 4.1 %collective-permute-done.7 = f32[1,130]{1,0:T(1,128)S(1)} collective-permute-done((f32[1,130]{1,0:T(1,128)S(1)}, f32[1,130]{1,0:T(1,128)S(1)}, u32[]{:S(2)}, u32[]{:S(2)}) %collective-permute-start.7) | collective-permute-done | bytes 552 | tf_op jit(solution)/shard_map/ppermute | solution.py:22
  33.7 37.2 %all-reduce.3 = (f32[]{:T(128)}, f32[]{:T(128)}) all-reduce(f32[]{:T(128)} %get-tuple-element.13, f32[]{:T(128)} %get-tuple-element.12), channel_id=1, replica_groups=mesh['lon'=8,'lat'=4] {'lon','lat'}, use_global_device_ids=true, to_apply=%region_1.0 | all-reduce | flops 2 | bytes 16 | tf_op jit(solution)/shard_map/psum | solution.py:117
  72.4 2.6 collective-permute-start.8
  75.0 1.4 collective-permute-done.9
  76.5 2.3 collective-permute-start.10
  79.3 1.5 collective-permute-done.10
  80.8 3.3 %collective-permute-done.11 = f32[1,130]{1,0:T(1,128)S(1)} collective-permute-done((f32[1,130]{1,0:T(1,128)S(1)}, f32[1,130]{1,0:T(1,128)S(1)}, u32[]{:S(2)}, u32[]{:S(2)}) %collective-permute-start.11) | collective-permute-done | bytes 552 | tf_op jit(solution)/shard_map/ppermute | solution.py:22
  84.1 0.8 multiply_reduce_fusion.4
  84.9 38.5 %all-reduce.2 = (f32[]{:T(128)}, f32[]{:T(128)}) all-reduce(f32[]{:T(128)} %get-tuple-element.11, f32[]{:T(128)} %get-tuple-element.10), channel_id=1, replica_groups=mesh['lon'=8,'lat'=4] {'lon','lat'}, use_global_device_ids=true, to_apply=%region_5.0 | all-reduce | flops 2 | bytes 16 | tf_op jit(solution)/shard_map/psum | solution.py:117
  128.0 2.6 collective-permute-start.12
  130.7 1.4 collective-permute-done.13
  132.1 2.3 collective-permute-start.14
  134.9 1.4 collective-permute-done.14
  136.3 3.5 %collective-permute-done.15 = f32[1,130]{1,0:T(1,128)S(1)} collective-permute-done((f32[1,130]{1,0:T(1,128)S(1)}, f32[1,130]{1,0:T(1,128)S(1)}, u32[]{:S(2)}, u32[]{:S(2)}) %collective-permute-start.15) | collective-permute-done | bytes 552 | tf_op jit(solution)/shard_map/ppermute | solution.py:22
  140.5 38.1 %all-reduce.1 = (f32[]{:T(128)}, f32[]{:T(128)}) all-reduce(f32[]{:T(128)} %get-tuple-element.9, f32[]{:T(128)} %get-tuple-element.8), channel_id=1, replica_groups=mesh['lon'=8,'lat'=4] {'lon','lat'}, use_global_device_ids=true, to_apply=%region_9.0 | all-reduce | flops 2 | bytes 16 | tf_op jit(solution)/shard_map/psum | solution.py:117
  182.3 2.6 collective-permute-start.16
  184.9 1.4 collective-permute-done.17
  186.4 2.3 collective-permute-start.18
  189.2 3.2 %slice_multiply_fusion.3 = (f32[40,26,130]{2,0,1:T(8,128)}, f32[40,26,130]{2,0,1:T(8,128)}, f32[40,26,130]{2,0,1:T(8,128)}, f32[40,26,130]{2,0,1:T(8,128)}) fusion(f32[40,28,132]{2,0,1:T(8,128)S(1)} %fusion.29), kind=kLoop, calls=%fused_computation.51 | loop fusion | flops 540800 | bytes 4867200 | tf_op jit(solution)/shard_map/mul | solution.py:70
  192.4 1.7 collective-permute-done.19
  194.1 1.3 multiply_reduce_fusion
  195.4 39.5 %all-reduce = (f32[]{:T(128)}, f32[]{:T(128)}) all-reduce(f32[]{:T(128)} %get-tuple-element.7, f32[]{:T(128)} %get-tuple-element.6), channel_id=1, replica_groups=mesh['lon'=8,'lat'=4] {'lon','lat'}, use_global_device_ids=true, to_apply=%region_13.0 | all-reduce | flops 2 | bytes 16 | tf_op jit(solution)/shard_map/psum | solution.py:117
  238.7 2.9 copy.9
  241.6 2.0 copy.11
  243.6 1.6 pad_maximum_fusion.9
  245.2 1.6 collective-permute-start.23
  247.9 7.0 %collective-permute-done.23 = f32[4,40,2,132]{3,1,2,0:T(8,128)S(1)} collective-permute-done((f32[4,40,2,132]{3,1,2,0:T(8,128)S(1)}, f32[4,40,2,132]{3,1,2,0:T(8,128)S(1)}, u32[]{:S(2)}, u32[]{:S(2)}) %collective-permute-start.23) | collective-permute-done | bytes 168992 | tf_op jit(solution)/shard_map/ppermute | solution.py:24
  255.0 7.6 %collective-permute-done.22 = f32[4,40,2,132]{3,1,2,0:T(8,128)S(1)} collective-permute-done((f32[4,40,2,132]{3,1,2,0:T(8,128)S(1)}, f32[4,40,2,132]{3,1,2,0:T(8,128)S(1)}, u32[]{:S(2)}, u32[]{:S(2)}) %collective-permute-start.22) | collective-permute-done | bytes 168992 | tf_op jit(solution)/shard_map/ppermute | solution.py:22
  262.6 0.7 copy-done.7
  263.3 2.1 pad_maximum_fusion
  266.0 1.6 fusion.33
  267.6 2.9 fusion.75
  270.6 11.5 %fusion.2 = f32[4,40,26,130]{3,1,2,0:T(8,128)} fusion(f32[4,40,2,132]{3,1,2,0:T(8,128)} %copy-done.7, f32[4,40,24,2]{3,1,2,0:T(8,128)S(1)} %copy-done.1, f32[4,40,24,128]{3,1,2,0:T(8,128)S(1)} %copy.10, f32[4,40,24,2]{3,1,2,0:T(8,128)S(1)} %copy-done, f32[4,40,2,132]{3,1,2,0:T(8,128)} %copy-done.5, f32[4,40,28,132]{3,1,2,0:T(8,128)S(1)} %pad_maximum_fusion, ...), kind=kLoop, calls=%fused_computation.4 | loop fusion | flops 9193600 | bytes 13181440 | tf_op jit(solution)/shard_map/sub | solution.py:74
  282.1 12.6 %fusion.13 = f32[4,40,24,128]{3,1,2,0:T(8,128)} fusion(f32[4,40,26,130]{3,1,2,0:T(8,128)} %fusion.2, f32[4,40,24,128]{3,1,2,0:T(8,128)S(1)} %copy.10, f32[4,40,2,132]{3,1,2,0:T(8,128)S(1)} %copy-done.8, f32[4,40,24,2]{3,1,2,0:T(8,128)} %copy.11, f32[4,40,24,2]{3,1,2,0:T(8,128)S(1)} %copy-done, f32[4,40,2,132]{3,1,2,0:T(8,128)S(1)} %copy-done.6, ...), kind=kLoop, calls=%fused_computation.23 | loop fusion | flops 16711680 | bytes 18585600 | tf_op jit(solution)/shard_map/mul | solution.py:108
  294.7 3.2 %copy.20 = f32[4,40,24,128]{3,2,1,0:T(8,128)} copy(f32[4,40,24,128]{3,1,2,0:T(8,128)} %fusion.13) | data formatting | bytes 3932160
  (76 shorter events, 6.4 us)
Async XLA Ops:
  1.5 11.9 %collective-permute-start = (s32[2,24,2]{2,1,0:T(8,128)S(1)}, s32[2,24,2]{2,1,0:T(8,128)S(1)}, u32[]{:S(2)}, u32[]{:S(2)}) collective-permute-start(s32[2,24,2]{2,1,0:T(8,128)S(1)} %get-tuple-element.71), channel_id=1, source_target_pairs={{0,4},{4,8},{8,12},{12,16},{16,20},{20,24},{24,28},{28,0},{1,5},{5... | collective-permute-start | bytes 1160 | tf_op jit(solution)/shard_map/ppermute | solution.py:22
  2.0 11.4 %collective-permute-start.1 = (s32[2,24,2]{2,1,0:T(8,128)S(1)}, s32[2,24,2]{2,1,0:T(8,128)S(1)}, u32[]{:S(2)}, u32[]{:S(2)}) collective-permute-start(s32[2,24,2]{2,1,0:T(8,128)S(1)} %get-tuple-element.72), channel_id=1, source_target_pairs={{4,0},{8,4},{12,8},{16,12},{20,16},{24,20},{28,24},{0,28},{5,1},{9... | collective-permute-start | bytes 1160 | tf_op jit(solution)/shard_map/ppermute | solution.py:24
  9.0 4.4 %copy-start.10 = (s32[24,128]{1,0:T(8,128)S(1)}, s32[24,128]{1,0:T(8,128)}, u32[]{:S(2)}) copy-start(s32[24,128]{1,0:T(8,128)} %param.6) | copy-start | bytes 36868
  9.0 4.4 %copy-start.11 = (s32[24,128]{1,0:T(8,128)S(1)}, s32[24,128]{1,0:T(8,128)}, u32[]{:S(2)}) copy-start(s32[24,128]{1,0:T(8,128)} %param.5) | copy-start | bytes 36868
  11.3 230.3 %collective-permute-start.21 = (f32[4,40,24,2]{1,2,3,0:T(8,128)S(1)}, f32[4,40,24,2]{1,2,3,0:T(8,128)S(1)}, u32[]{:S(2)}, u32[]{:S(2)}) collective-permute-start(f32[4,40,24,2]{1,2,3,0:T(8,128)S(1)} %copy.22), channel_id=1, source_target_pairs={{4,0},{8,4},{12,8},{16,12},{20,16},{24,20},{28,24},{0,28},{5,1},{9... | collective-permute-start | bytes 92168 | tf_op jit(solution)/shard_map/ppermute | solution.py:24
  13.4 225.3 %collective-permute-start.20 = (f32[4,40,24,2]{1,2,3,0:T(8,128)}, f32[4,40,24,2]{1,2,3,0:T(8,128)}, u32[]{:S(2)}, u32[]{:S(2)}) collective-permute-start(f32[4,40,24,2]{1,2,3,0:T(8,128)} %copy.21), channel_id=1, source_target_pairs={{0,4},{4,8},{8,12},{12,16},{16,20},{20,24},{24,28},{28,0},{1,5},{5... | collective-permute-start | bytes 92168 | tf_op jit(solution)/shard_map/ppermute | solution.py:22
  13.5 6.2 %collective-permute-start.2 = (s32[2,2,132]{2,1,0:T(2,128)S(1)}, s32[2,2,132]{2,1,0:T(2,128)S(1)}, u32[]{:S(2)}, u32[]{:S(2)}) collective-permute-start(s32[2,2,132]{2,1,0:T(2,128)S(1)} %get-tuple-element.61), channel_id=1, source_target_pairs={{0,1},{1,2},{2,3},{3,0},{4,5},{5,6},{6,7},{7,4},{8,9},{9,10},{10,1... | collective-permute-start | bytes 6344 | tf_op jit(solution)/shard_map/ppermute | solution.py:22
  15.7 4.0 %collective-permute-start.3 = (s32[2,2,132]{2,1,0:T(2,128)S(1)}, s32[2,2,132]{2,1,0:T(2,128)S(1)}, u32[]{:S(2)}, u32[]{:S(2)}) collective-permute-start(s32[2,2,132]{2,1,0:T(2,128)S(1)} %get-tuple-element.62), channel_id=1, source_target_pairs={{1,0},{2,1},{3,2},{0,3},{5,4},{6,5},{7,6},{4,7},{9,8},{10,9},{11,1... | collective-permute-start | bytes 6344 | tf_op jit(solution)/shard_map/ppermute | solution.py:24
  17.8 2.1 copy-start.12
  20.0 4.0 %collective-permute-start.5 = (f32[24,1]{1,0:T(8,128)S(1)}, f32[24,1]{1,0:T(8,128)S(1)}, u32[]{:S(2)}, u32[]{:S(2)}) collective-permute-start(f32[24,1]{1,0:T(8,128)S(1)} %get-tuple-element.79), channel_id=1, source_target_pairs={{0,4},{4,8},{8,12},{12,16},{16,20},{20,24},{24,28},{28,0},{1,5},{5... | collective-permute-start | bytes 296 | tf_op jit(solution)/shard_map/ppermute | solution.py:22
  20.1 4.0 %collective-permute-start.4 = (f32[24,1]{1,0:T(8,128)S(1)}, f32[24,1]{1,0:T(8,128)S(1)}, u32[]{:S(2)}, u32[]{:S(2)}) collective-permute-start(f32[24,1]{1,0:T(8,128)S(1)} %get-tuple-element.80), channel_id=1, source_target_pairs={{4,0},{8,4},{12,8},{16,12},{20,16},{24,20},{28,24},{0,28},{5,1},{9... | collective-permute-start | bytes 296 | tf_op jit(solution)/shard_map/ppermute | solution.py:24
  24.2 4.8 %collective-permute-start.6 = (f32[1,130]{1,0:T(1,128)S(1)}, f32[1,130]{1,0:T(1,128)S(1)}, u32[]{:S(2)}, u32[]{:S(2)}) collective-permute-start(f32[1,130]{1,0:T(1,128)S(1)} %get-tuple-element.69), channel_id=1, source_target_pairs={{1,0},{2,1},{3,2},{0,3},{5,4},{6,5},{7,6},{4,7},{9,8},{10,9},{11,1... | collective-permute-start | bytes 1568 | tf_op jit(solution)/shard_map/ppermute | solution.py:24
  27.6 5.4 %collective-permute-start.7 = (f32[1,130]{1,0:T(1,128)S(1)}, f32[1,130]{1,0:T(1,128)S(1)}, u32[]{:S(2)}, u32[]{:S(2)}) collective-permute-start(f32[1,130]{1,0:T(1,128)S(1)} %get-tuple-element.70), channel_id=1, source_target_pairs={{0,1},{1,2},{2,3},{3,0},{4,5},{5,6},{6,7},{7,4},{8,9},{9,10},{10,1... | collective-permute-start | bytes 1568 | tf_op jit(solution)/shard_map/ppermute | solution.py:22
  72.4 4.0 %collective-permute-start.9 = (f32[24,1]{1,0:T(8,128)S(1)}, f32[24,1]{1,0:T(8,128)S(1)}, u32[]{:S(2)}, u32[]{:S(2)}) collective-permute-start(f32[24,1]{1,0:T(8,128)S(1)} %get-tuple-element.77), channel_id=1, source_target_pairs={{0,4},{4,8},{8,12},{12,16},{16,20},{20,24},{24,28},{28,0},{1,5},{5... | collective-permute-start | bytes 296 | tf_op jit(solution)/shard_map/ppermute | solution.py:22
  72.4 4.1 %collective-permute-start.8 = (f32[24,1]{1,0:T(8,128)S(1)}, f32[24,1]{1,0:T(8,128)S(1)}, u32[]{:S(2)}, u32[]{:S(2)}) collective-permute-start(f32[24,1]{1,0:T(8,128)S(1)} %get-tuple-element.78), channel_id=1, source_target_pairs={{4,0},{8,4},{12,8},{16,12},{20,16},{24,20},{28,24},{0,28},{5,1},{9... | collective-permute-start | bytes 296 | tf_op jit(solution)/shard_map/ppermute | solution.py:24
  76.5 4.3 %collective-permute-start.10 = (f32[1,130]{1,0:T(1,128)S(1)}, f32[1,130]{1,0:T(1,128)S(1)}, u32[]{:S(2)}, u32[]{:S(2)}) collective-permute-start(f32[1,130]{1,0:T(1,128)S(1)} %get-tuple-element.67), channel_id=1, source_target_pairs={{1,0},{2,1},{3,2},{0,3},{5,4},{6,5},{7,6},{4,7},{9,8},{10,9},{11,1... | collective-permute-start | bytes 1568 | tf_op jit(solution)/shard_map/ppermute | solution.py:24
  78.8 5.4 %collective-permute-start.11 = (f32[1,130]{1,0:T(1,128)S(1)}, f32[1,130]{1,0:T(1,128)S(1)}, u32[]{:S(2)}, u32[]{:S(2)}) collective-permute-start(f32[1,130]{1,0:T(1,128)S(1)} %get-tuple-element.68), channel_id=1, source_target_pairs={{0,1},{1,2},{2,3},{3,0},{4,5},{5,6},{6,7},{7,4},{8,9},{9,10},{10,1... | collective-permute-start | bytes 1568 | tf_op jit(solution)/shard_map/ppermute | solution.py:22
  128.0 4.0 %collective-permute-start.13 = (f32[24,1]{1,0:T(8,128)S(1)}, f32[24,1]{1,0:T(8,128)S(1)}, u32[]{:S(2)}, u32[]{:S(2)}) collective-permute-start(f32[24,1]{1,0:T(8,128)S(1)} %get-tuple-element.75), channel_id=1, source_target_pairs={{0,4},{4,8},{8,12},{12,16},{16,20},{20,24},{24,28},{28,0},{1,5},{5... | collective-permute-start | bytes 296 | tf_op jit(solution)/shard_map/ppermute | solution.py:22
  128.0 4.0 %collective-permute-start.12 = (f32[24,1]{1,0:T(8,128)S(1)}, f32[24,1]{1,0:T(8,128)S(1)}, u32[]{:S(2)}, u32[]{:S(2)}) collective-permute-start(f32[24,1]{1,0:T(8,128)S(1)} %get-tuple-element.76), channel_id=1, source_target_pairs={{4,0},{8,4},{12,8},{16,12},{20,16},{24,20},{28,24},{0,28},{5,1},{9... | collective-permute-start | bytes 296 | tf_op jit(solution)/shard_map/ppermute | solution.py:24
  132.1 4.1 %collective-permute-start.14 = (f32[1,130]{1,0:T(1,128)S(1)}, f32[1,130]{1,0:T(1,128)S(1)}, u32[]{:S(2)}, u32[]{:S(2)}) collective-permute-start(f32[1,130]{1,0:T(1,128)S(1)} %get-tuple-element.65), channel_id=1, source_target_pairs={{1,0},{2,1},{3,2},{0,3},{5,4},{6,5},{7,6},{4,7},{9,8},{10,9},{11,1... | collective-permute-start | bytes 1568 | tf_op jit(solution)/shard_map/ppermute | solution.py:24
  134.4 5.4 %collective-permute-start.15 = (f32[1,130]{1,0:T(1,128)S(1)}, f32[1,130]{1,0:T(1,128)S(1)}, u32[]{:S(2)}, u32[]{:S(2)}) collective-permute-start(f32[1,130]{1,0:T(1,128)S(1)} %get-tuple-element.66), channel_id=1, source_target_pairs={{0,1},{1,2},{2,3},{3,0},{4,5},{5,6},{6,7},{7,4},{8,9},{9,10},{10,1... | collective-permute-start | bytes 1568 | tf_op jit(solution)/shard_map/ppermute | solution.py:22
  182.2 11.9 %copy-start.13 = (f32[24,128]{1,0:T(8,128)}, f32[24,128]{1,0:T(8,128)S(1)}, u32[]{:S(2)}) copy-start(f32[24,128]{1,0:T(8,128)S(1)} %get-tuple-element.24) | copy-start | bytes 36868
  182.3 4.0 %collective-permute-start.17 = (f32[24,1]{1,0:T(8,128)S(1)}, f32[24,1]{1,0:T(8,128)S(1)}, u32[]{:S(2)}, u32[]{:S(2)}) collective-permute-start(f32[24,1]{1,0:T(8,128)S(1)} %get-tuple-element.73), channel_id=1, source_target_pairs={{0,4},{4,8},{8,12},{12,16},{16,20},{20,24},{24,28},{28,0},{1,5},{5... | collective-permute-start | bytes 296 | tf_op jit(solution)/shard_map/ppermute | solution.py:22
  182.3 4.0 %collective-permute-start.16 = (f32[24,1]{1,0:T(8,128)S(1)}, f32[24,1]{1,0:T(8,128)S(1)}, u32[]{:S(2)}, u32[]{:S(2)}) collective-permute-start(f32[24,1]{1,0:T(8,128)S(1)} %get-tuple-element.74), channel_id=1, source_target_pairs={{4,0},{8,4},{12,8},{16,12},{20,16},{24,20},{28,24},{0,28},{5,1},{9... | collective-permute-start | bytes 296 | tf_op jit(solution)/shard_map/ppermute | solution.py:24
  186.4 5.9 %collective-permute-start.18 = (f32[1,130]{1,0:T(1,128)S(1)}, f32[1,130]{1,0:T(1,128)S(1)}, u32[]{:S(2)}, u32[]{:S(2)}) collective-permute-start(f32[1,130]{1,0:T(1,128)S(1)} %get-tuple-element.63), channel_id=1, source_target_pairs={{1,0},{2,1},{3,2},{0,3},{5,4},{6,5},{7,6},{4,7},{9,8},{10,9},{11,1... | collective-permute-start | bytes 1568 | tf_op jit(solution)/shard_map/ppermute | solution.py:24
  188.7 5.4 %collective-permute-start.19 = (f32[1,130]{1,0:T(1,128)S(1)}, f32[1,130]{1,0:T(1,128)S(1)}, u32[]{:S(2)}, u32[]{:S(2)}) collective-permute-start(f32[1,130]{1,0:T(1,128)S(1)} %get-tuple-element.64), channel_id=1, source_target_pairs={{0,1},{1,2},{2,3},{3,0},{4,5},{5,6},{6,7},{7,4},{8,9},{9,10},{10,1... | collective-permute-start | bytes 1568 | tf_op jit(solution)/shard_map/ppermute | solution.py:22
  243.6 3.7 %copy-start.14 = (f32[24,128]{1,0:T(8,128)S(1)}, f32[24,128]{1,0:T(8,128)}, u32[]{:S(2)}) copy-start(f32[24,128]{1,0:T(8,128)} %copy-done.13) | copy-start | bytes 36868
  243.6 3.7 %copy-start.15 = (f32[24,128]{1,0:T(8,128)S(1)}, f32[24,128]{1,0:T(8,128)}, u32[]{:S(2)}) copy-start(f32[24,128]{1,0:T(8,128)} %get-tuple-element.22) | copy-start | bytes 36868
  243.6 19.7 %copy-start = (f32[4,40,24,2]{3,1,2,0:T(8,128)S(1)}, f32[4,40,24,2]{3,1,2,0:T(8,128)}, u32[]{:S(2)}) copy-start(f32[4,40,24,2]{3,1,2,0:T(8,128)} %copy.9) | copy-start | bytes 92164
  243.6 19.7 %copy-start.1 = (f32[4,40,24,2]{3,1,2,0:T(8,128)S(1)}, f32[4,40,24,2]{3,1,2,0:T(8,128)}, u32[]{:S(2)}) copy-start(f32[4,40,24,2]{3,1,2,0:T(8,128)} %copy.11) | copy-start | bytes 92164
  245.2 9.7 %collective-permute-start.23 = (f32[4,40,2,132]{3,1,2,0:T(8,128)S(1)}, f32[4,40,2,132]{3,1,2,0:T(8,128)S(1)}, u32[]{:S(2)}, u32[]{:S(2)}) collective-permute-start(f32[4,40,2,132]{3,1,2,0:T(8,128)S(1)} %get-tuple-element.40), channel_id=1, source_target_pairs={{1,0},{2,1},{3,2},{0,3},{5,4},{6,5},{7,6},{4,7},{9,8},{10,9},{11,1... | collective-permute-start | bytes 506888 | tf_op jit(solution)/shard_map/ppermute | solution.py:24
  246.8 15.7 %collective-permute-start.22 = (f32[4,40,2,132]{3,1,2,0:T(8,128)S(1)}, f32[4,40,2,132]{3,1,2,0:T(8,128)S(1)}, u32[]{:S(2)}, u32[]{:S(2)}) collective-permute-start(f32[4,40,2,132]{3,1,2,0:T(8,128)S(1)} %get-tuple-element.41), channel_id=1, source_target_pairs={{0,1},{1,2},{2,3},{3,0},{4,5},{5,6},{6,7},{7,4},{8,9},{9,10},{10,1... | collective-permute-start | bytes 506888 | tf_op jit(solution)/shard_map/ppermute | solution.py:22
  255.0 7.6 %copy-start.5 = (f32[4,40,2,132]{3,1,2,0:T(8,128)}, f32[4,40,2,132]{3,1,2,0:T(8,128)S(1)}, u32[]{:S(2)}) copy-start(f32[4,40,2,132]{3,1,2,0:T(8,128)S(1)} %collective-permute-done.23) | copy-start | bytes 506884
  262.6 0.7 copy-start.7
  267.6 2.9 copy-start.2
  267.6 2.9 copy-start.3
  267.6 2.9 copy-start.4
  270.5 11.5 %copy-start.6 = (f32[4,40,2,132]{3,1,2,0:T(8,128)S(1)}, f32[4,40,2,132]{3,1,2,0:T(8,128)}, u32[]{:S(2)}) copy-start(f32[4,40,2,132]{3,1,2,0:T(8,128)} %copy-done.5) | copy-start | bytes 506884
  270.5 11.5 %copy-start.8 = (f32[4,40,2,132]{3,1,2,0:T(8,128)S(1)}, f32[4,40,2,132]{3,1,2,0:T(8,128)}, u32[]{:S(2)}) copy-start(f32[4,40,2,132]{3,1,2,0:T(8,128)} %copy-done.7) | copy-start | bytes 506884
  270.5 11.5 %copy-start.9 = (f32[40,24,128]{2,0,1:T(8,128)S(1)}, f32[40,24,128]{2,0,1:T(8,128)}, u32[]{:S(2)}) copy-start(f32[40,24,128]{2,0,1:T(8,128)} %get-tuple-element.50) | copy-start | bytes 1474564
where the time goes:
time: 299 us; the launch traced here: 298 us
  blocking collectives  153 us (51%)
  other arithmetic  41.4 us (14%)
  waiting for transfers between devices  37 us (12%)
  starting transfers between devices  32.7 us (11%)
  local copies, waits for them, and re-layouts  19.4 us (6%)
  between operations  14.1 us (5%)
    psum x4, blocking collectives, paired_totals(): lax.psum((jnp.sum(trim_rims(residual * search, width)), jnp.sum(trim_rims...  153 us
    ppermute x12, starting transfers between devices, with_halo(): lax.ppermute(head, axis, [((i + 1) % count, i) for i in range(count)])  28.2 us
    ppermute x12, waiting for transfers between devices, with_halo(): lax.ppermute(tail, axis, [(i, (i + 1) % count) for i in range(count)])  25.7 us
    mul x1, other arithmetic, tendency_of(): return trim_rims(active_wide, 2) * (-flux - viscosity * smoothed)  12.6 us
    sub x1, other arithmetic, laplace(): return east_part - west_part + north_part - south_part  11.5 us
    ppermute x12, waiting for transfers between devices, with_halo(): lax.ppermute(head, axis, [((i + 1) % count, i) for i in range(count)])  11.3 us
    unnamed x36, local copies, waits for them, and re-layouts  9.51 us
  transfers between devices with their start and end apart: 24, of which 13 were waited for; matrix products, arithmetic and copies ran while one was open for 7% of the time, Pallas kernels for 0%

commit v1 on v0

v1 whole, which is shorter than its diff:
```python
import functools

import jax
import jax.numpy as jnp
from jax import lax
from jax.experimental import pallas as pl
from jax.experimental.pallas import tpu as pltpu
from jax.sharding import PartitionSpec as P

ITERS = 4
DAMPING = 0.05
VISCOSITY = 0.02
COLS = 4
MESH = pl.DeviceIdType.MESH


def east(a, b, lane):
    ra, rb = pltpu.roll(a, 127, 1), pltpu.roll(b, 127, 1)
    keep = lane < 127
    return jnp.where(keep, ra, rb), jnp.where(keep, rb, ra)


def west(a, b, lane):
    ra, rb = pltpu.roll(a, 1, 1), pltpu.roll(b, 1, 1)
    keep = lane > 0
    return jnp.where(keep, ra, rb), jnp.where(keep, rb, ra)


def north(x):
    return pltpu.roll(x, x.shape[0] - 1, 0)


def south(x):
    return pltpu.roll(x, 1, 0)


def lanes(x):
    return lax.broadcasted_iota(jnp.int32, x.shape, 1)


def kernel(
    sizes,
    forcing_ref, sea_ref, count_ref, state_ref,
    height_ref, resid_ref, tend_ref,
    q_ref, o_ref, side_ref, vert_ref,
    rows_out, rows_in, cols_out, cols_in, corner_out, corner_in, strip_ref, wet_ref,
    basis_ref, diag_ref, part_ref, lon_in, mid_ref, lat_in,
    load_sem, store_sem,
    side_sem, vert_sem, row_sem, col_sem, corner_sem, lon_sem, lat_sem,
):
    n_lon, n_lat, fields, levels, rows = sizes
    planes = fields * levels
    groups = strip_ref.shape[0] // 32
    per_group = 128 // COLS
    ilon, ilat = lax.axis_index("lon"), lax.axis_index("lat")

    def at(dlon, dlat):
        return {
            "lon": lax.rem(ilon + dlon + n_lon, n_lon),
            "lat": lax.rem(ilat + dlat + n_lat, n_lat),
        }

    load = pltpu.make_async_copy(state_ref, q_ref, load_sem)
    load.start()

    barrier = pltpu.get_barrier_semaphore()
    diagonals = [(-1, -1), (1, -1), (-1, 1), (1, 1)]
    for off in range(1, n_lon):
        pl.semaphore_signal(barrier, inc=1, device_id=at(off, 0), device_id_type=MESH)
    for off in range(1, n_lat):
        pl.semaphore_signal(barrier, inc=1, device_id=at(0, off), device_id_type=MESH)
    for dlon, dlat in diagonals:
        pl.semaphore_signal(barrier, inc=1, device_id=at(dlon, dlat), device_id_type=MESH)
    pl.semaphore_wait(barrier, n_lon + n_lat + 2)

    def send(src, dst, sems, index, where):
        copy = pltpu.make_async_remote_copy(
            src_ref=src, dst_ref=dst, send_sem=sems.at[0, index], recv_sem=sems.at[1, index],
            device_id=where, device_id_type=MESH,
        )
        copy.start()
        return copy

    surface = (forcing_ref, sea_ref, count_ref)
    surface_copies = []
    for side, dlon in ((0, 1), (1, -1)):
        for i, ref in enumerate(surface):
            surface_copies.append(send(ref, side_ref.at[i, side], side_sem, i * 2 + side, at(dlon, 0)))
    for v, dlat in ((0, -1), (1, 1)):
        part = pl.ds(0, 8) if v == 0 else pl.ds(rows - 8, 8)
        for h, dlon in ((0, 1), (1, 0), (2, -1)):
            for i, ref in enumerate(surface):
                surface_copies.append(
                    send(ref.at[part], vert_ref.at[i, v, h], vert_sem, (i * 2 + v) * 3 + h, at(dlon, dlat))
                )

    load.wait()
    for i, j in enumerate((0, 1, rows - 2, rows - 1)):
        rows_out[i] = q_ref[pl.ds(j, planes, stride=rows), :]
    state_copies = [
        send(rows_out.at[pl.ds(2, 2)], rows_in.at[pl.ds(0, 2)], row_sem, 0, at(0, 1)),
        send(rows_out.at[pl.ds(0, 2)], rows_in.at[pl.ds(2, 2)], row_sem, 1, at(0, -1)),
    ]

    lane_r = lax.broadcasted_iota(jnp.int32, (rows, 128), 1)
    for g in range(groups):
        inside = min(per_group, planes - g * per_group)

        def pack(s, acc, g=g):
            plane = q_ref[pl.ds(pl.multiple_of((g * per_group + s) * rows, 8), rows), :]
            moved = pltpu.roll(plane, lax.rem(COLS * s + 2, 128), 1)
            return jnp.where(lane_r // COLS == s, moved, acc)

        cols_out[pl.ds(g * rows, rows), :] = lax.fori_loop(
            0, inside, pack, jnp.zeros((rows, 128), jnp.float32), unroll=4
        )
    for i, j in enumerate((0, rows - 1)):
        for g in range(groups):
            corner_out[i, pl.ds(g, 1), :] = cols_out[pl.ds(g * rows + j, 1), :]
    state_copies += [
        send(cols_out, cols_in.at[0], col_sem, 0, at(1, 0)),
        send(cols_out, cols_in.at[1], col_sem, 1, at(-1, 0)),
    ]
    for v, dlat in ((0, -1), (1, 1)):
        for h, dlon in ((0, 1), (1, -1)):
            state_copies.append(
                send(corner_out.at[v], corner_in.at[v, h], corner_sem, v * 2 + h, at(dlon, dlat))
            )

    for copy in surface_copies:
        copy.wait()
    lane8 = lax.broadcasted_iota(jnp.int32, (8, 128), 1)
    above = jnp.where(ilat < n_lat - 1, 1.0, 0.0).astype(jnp.float32)
    below = jnp.where(ilat > 0, 1.0, 0.0).astype(jnp.float32)

    def torus(i):
        ref = surface[i]
        a = jnp.concatenate([ref[...], vert_ref[i, 0, 1], vert_ref[i, 1, 1]], axis=0)
        b = jnp.concatenate(
            [
                jnp.where(lane_r < 64, side_ref[i, 1], side_ref[i, 0]),
                jnp.where(lane8 < 64, vert_ref[i, 0, 2], vert_ref[i, 0, 0]),
                jnp.where(lane8 < 64, vert_ref[i, 1, 2], vert_ref[i, 1, 0]),
            ],
            axis=0,
        )
        return a, b

    row_t = lax.broadcasted_iota(jnp.int32, (rows + 16, 128), 0)
    lane_t = lax.broadcasted_iota(jnp.int32, (rows + 16, 128), 1)
    valid = jnp.where(row_t < rows, 1.0, jnp.where(row_t < rows + 8, above, below))

    force_a, force_b = torus(0)
    sea_a, sea_b = (x * valid for x in torus(1))
    count_a, count_b = torus(2)
    wet_a, wet_b = sea_a * count_a, sea_b * count_b
    sub8 = lax.broadcasted_iota(jnp.int32, (8, 128), 0)
    for i, wet in enumerate((wet_a, wet_b)):
        wet_ref[i, pl.ds(0, rows), :] = wet[:rows]
        wet_ref[i, pl.ds(rows, 8), :] = jnp.where(sub8 < 4, wet[rows : rows + 8], wet[rows + 8 :])
    depth_a, depth_b = wet_a / levels, wet_b / levels
    da, db = east(depth_a, depth_b, lane_t)
    ea, eb = jnp.minimum(depth_a, da), jnp.minimum(depth_b, db)
    wa, wb = west(ea, eb, lane_t)
    na, nb = jnp.minimum(depth_a, north(depth_a)), jnp.minimum(depth_b, north(depth_b))
    sa, sb = south(na), south(nb)
    diag_a = DAMPING + ea + wa + na + sa
    diag_b = DAMPING + eb + wb + nb + sb
    inv_a, inv_b = 1.0 / diag_a, 1.0 / diag_b
    va, vb = sea_a * force_a * inv_a, sea_b * force_b * inv_b
    ea, wa, na, sa = (c * inv_a for c in (ea, wa, na, sa))
    eb, wb, nb, sb = (c * inv_b for c in (eb, wb, nb, sb))
    diag = diag_a[:rows]
    diag_ref[...] = diag
    basis = [va[:rows]]
    for _ in range(ITERS):
        qe, qeb = east(va, vb, lane_t)
        qw, qwb = west(va, vb, lane_t)
        va, vb = (
            ea * qe + wa * qw + na * north(va) + sa * south(va),
            eb * qeb + wb * qwb + nb * north(vb) + sb * south(vb),
        )
        basis.append(va[:rows])
    for i, v in enumerate(basis):
        basis_ref[i] = v
    moments = []
    for m in range(2 * ITERS):
        moments.append(jnp.sum(diag * basis[m // 2] * basis[(m + 1) // 2], axis=0, keepdims=True))
    part_ref[...] = jnp.concatenate(moments, axis=0)
    lon_copies = [
        send(part_ref, lon_in.at[off - 1], lon_sem, off - 1, at(off, 0)) for off in range(1, n_lon)
    ]

    for copy in state_copies:
        copy.wait()
    left_slot = lane_r % COLS < 2
    left8 = lane8 % COLS < 2
    for g in range(groups):
        span = pl.ds(g * rows, rows)
        strip_ref[pl.ds(g * 32, rows), :] = jnp.where(left_slot, cols_in[0, span, :], cols_in[1, span, :])
        one = pl.ds(g, 1)
        up = jnp.where(left8[:1], corner_in[0, 0, one, :], corner_in[0, 1, one, :])
        down = jnp.where(left8[:1], corner_in[1, 0, one, :], corner_in[1, 1, one, :])
        strip_ref[pl.ds(g * 32 + rows, 8), :] = jnp.where(sub8 < 4, up, down)

    tall = rows + 8
    lane = lax.broadcasted_iota(jnp.int32, (tall, 128), 1)

    def plane_of(n):
        body = q_ref[pl.ds(pl.multiple_of(n * rows, 8), rows), :]
        one = pl.ds(n, 1)
        rim = jnp.where(
            sub8 < 4,
            jnp.where(sub8 == 0, rows_in[2, one, :], rows_in[3, one, :]),
            jnp.where(sub8 == 6, rows_in[0, one, :], rows_in[1, one, :]),
        )
        a = jnp.concatenate([body, rim], axis=0)
        strip = strip_ref[pl.ds(pl.multiple_of(n // per_group * 32, 8), tall), :]
        b = pltpu.roll(strip, lax.rem(128 - (COLS * (n % per_group) + 2) + 128, 128), 1)
        return a, b

    def level(k, carry):
        kf = k.astype(jnp.float32)
        aa = jnp.where(kf < wet_ref[0], 1.0, 0.0)
        ab = jnp.where(kf < wet_ref[1], 1.0, 0.0)
        ae, be = east(aa, ab, lane)
        ae, be = aa * ae, ab * be
        an, bn = aa * north(aa), ab * north(ab)
        ua, ub = plane_of(2 * levels + k)
        ue, ueb = east(ua, ub, lane)
        ue, ueb = 0.25 * ae * (ua + ue), 0.25 * be * (ub + ueb)
        va, _ = plane_of(3 * levels + k)
        vn = 0.25 * an * (va + north(va))
        for f in range(fields):
            n = f * levels + k
            qa, qb = plane_of(n)
            qe, qeb = east(qa, qb, lane)
            qn, qnb = north(qa), north(qb)
            fx, fxb = ae * (qe - qa), be * (qeb - qb)
            fw, fwb = west(fx, fxb, lane)
            fy, fyb = an * (qn - qa), bn * (qnb - qb)
            la, lb = fx - fw + fy - south(fy), fxb - fwb + fyb - south(fyb)
            le, leb = east(la, lb, lane)
            gx = ue * (qa + qe) + VISCOSITY * ae * (le - la)
            gxb = ueb * (qb + qeb) + VISCOSITY * be * (leb - lb)
            gy = vn * (qa + qn) + VISCOSITY * an * (north(la) - la)
            gw, _ = west(gx, gxb, lane)
            total = aa * (gw - gx + south(gy) - gy)
            o_ref[pl.ds(pl.multiple_of(n * rows, 8), rows), :] = total[:rows]
        return carry

    half = levels // 2
    lax.fori_loop(0, half, level, 0)

    for copy in lon_copies:
        copy.wait()
    mid = part_ref[...]
    for i in range(n_lon - 1):
        mid = mid + lon_in[i]
    mid_ref[...] = mid
    lat_copies = [
        send(mid_ref, lat_in.at[off - 1], lat_sem, off - 1, at(0, off)) for off in range(1, n_lat)
    ]

    lax.fori_loop(half, levels, level, 0)

    store = pltpu.make_async_copy(o_ref, tend_ref, store_sem)
    store.start()

    for copy in lat_copies:
        copy.wait()
    total = mid_ref[...]
    for i in range(n_lat - 1):
        total = total + lat_in[i]
    total = jnp.broadcast_to(jnp.sum(total, axis=1, keepdims=True), (8, 128))
    mu = [total[m : m + 1] for m in range(2 * ITERS)]

    def inner(x, y):
        sums = [None] * (len(x) + len(y) - 1)
        for i, xi in enumerate(x):
            for j, yj in enumerate(y):
                sums[i + j] = xi * yj if sums[i + j] is None else sums[i + j] + xi * yj
        out = sums[0] * mu[0]
        for m in range(1, len(sums)):
            out = out + sums[m] * mu[m]
        return out

    one = jnp.ones((1, 128), jnp.float32)
    zero = jnp.zeros((1, 128), jnp.float32)
    z, p, h = [one], [one], []
    rz = mu[0]
    for it in range(ITERS):
        image = [hi - lo for hi, lo in zip(p + [zero], [zero] + p)]
        alpha = rz / inner(p, image)
        h = [x + alpha * y for x, y in zip(h + [zero], p)]
        z = [x - alpha * y for x, y in zip(z + [zero], image)]
        if it + 1 < ITERS:
            new = inner(z, z)
            beta = new / rz
            p = [x + beta * y for x, y in zip(z, p + [zero])]
            rz = new
    height = h[0] * basis_ref[0]
    for i in range(1, ITERS):
        height = height + h[i] * basis_ref[i]
    resid = z[0] * basis_ref[0]
    for i in range(1, ITERS + 1):
        resid = resid + z[i] * basis_ref[i]
    height_ref[...] = height
    resid_ref[...] = diag_ref[...] * resid
    store.wait()


def per_device(n_lon, n_lat, forcing, sea, count, state):
    fields, levels, rows, width = state.shape
    planes = fields * levels
    per_group = 128 // COLS
    groups = -(-planes // per_group)
    corner_rows = -(-groups // 8) * 8
    sizes = (n_lon, n_lat, fields, levels, rows)
    f32 = jnp.float32
    vmem = pl.BlockSpec(memory_space=pltpu.VMEM)
    hbm = pl.BlockSpec(memory_space=pl.ANY)
    dma = pltpu.SemaphoreType.DMA
    height, resid, tend = pl.pallas_call(
        functools.partial(kernel, sizes),
        out_shape=(
            jax.ShapeDtypeStruct((rows, width), f32),
            jax.ShapeDtypeStruct((rows, width), f32),
            jax.ShapeDtypeStruct((planes * rows, width), f32),
        ),
        in_specs=[vmem, vmem, vmem, hbm],
        out_specs=(vmem, vmem, hbm),
        scratch_shapes=[
            pltpu.VMEM((planes * rows, width), f32),
            pltpu.VMEM((planes * rows, width), f32),
            pltpu.VMEM((3, 2, rows, width), f32),
            pltpu.VMEM((3, 2, 3, 8, width), f32),
            pltpu.VMEM((4, planes, width), f32),
            pltpu.VMEM((4, planes, width), f32),
            pltpu.VMEM((groups * rows, width), f32),
            pltpu.VMEM((2, groups * rows, width), f32),
            pltpu.VMEM((2, corner_rows, width), f32),
            pltpu.VMEM((2, 2, corner_rows, width), f32),
            pltpu.VMEM((groups * 32, width), f32),
            pltpu.VMEM((2, rows + 8, width), f32),
            pltpu.VMEM((ITERS + 1, rows, width), f32),
            pltpu.VMEM((rows, width), f32),
            pltpu.VMEM((8, width), f32),
            pltpu.VMEM((n_lon - 1, 8, width), f32),
            pltpu.VMEM((8, width), f32),
            pltpu.VMEM((n_lat - 1, 8, width), f32),
            dma,
            dma,
            dma((2, 6)),
            dma((2, 18)),
            dma((2, 2)),
            dma((2, 2)),
            dma((2, 4)),
            dma((2, n_lon - 1)),
            dma((2, n_lat - 1)),
        ],
        compiler_params=pltpu.CompilerParams(collective_id=0, has_side_effects=True),
    )(forcing, sea.astype(f32), count.astype(f32), state.reshape(planes * rows, width))
    return height, resid, tend.reshape(state.shape)


def solution(mesh):
    return jax.shard_map(
        functools.partial(per_device, mesh.shape["lon"], mesh.shape["lat"]),
        mesh=mesh,
        in_specs=(P("lat", "lon"), P("lat", "lon"), P("lat", "lon"), P(None, None, "lat", "lon")),
        out_specs=(P("lat", "lon"), P("lat", "lon"), P(None, None, "lat", "lon")),
        check_vma=False,
    )
```

time: 299 us -> 46.3 us (0.15)
  blocking collectives: 153 us -> 0 us
  other arithmetic: 41.4 us -> 2.62 us
  waiting for transfers between devices: 37 us -> 0 us
  Pallas kernels: 0 us -> 36.9 us
  starting transfers between devices: 32.7 us -> 0 us
  local copies, waits for them, and re-layouts: 19.4 us -> 5.56 us
  between operations: 14.1 us -> 0.64 us
    psum x4 -> x0, blocking collectives: 153 us -> none  [paired_totals(): lax.psum((jnp.sum(trim_rims(residual * search, width)), jnp.sum(trim_rims...]
    ppermute x24 -> x0, waiting for transfers between devices: 37 us -> none  [the longest x12 25.7 us: with_halo(): lax.ppermute(tail, axis, [(i, (i + 1) % count) for i in range(count)])]
    pallas_call x0 -> x1, Pallas kernels: none -> 36.9 us  [per_device(): pl.pallas_call(functools.partial(kernel, sizes), out_shape=(jax.ShapeDtyp...]
    ppermute x24 -> x0, starting transfers between devices: 32.7 us -> none  [the longest x12 28.2 us: with_halo(): lax.ppermute(head, axis, [((i + 1) % count, i) for i in range(count)])]
    mul x5 -> x0, other arithmetic: 17.6 us -> none  [the longest x1 12.6 us: tendency_of(): return trim_rims(active_wide, 2) * (-flux - viscosity * smoothed)]
    sub x2 -> x0, other arithmetic: 12.1 us -> none  [the longest x1 11.5 us: laplace(): return east_part - west_part + north_part - south_part]
    ppermute x2 -> x0, local copies, waits for them, and re-layouts: 4.9 us -> none  [the longest x1 2.91 us: with_halo(): lax.ppermute(tail, axis, [(i, (i + 1) % count) for i in range(count)])]
    slice x5 -> x0, local copies, waits for them, and re-layouts: 4.38 us -> none  [with_halo(): lax.slice_in_dim(cells, cells.shape[dim] - width, cells.shape[dim], axis=...]
  transfers between devices with their start and end apart: 24 -> 0, of which waited for: 13 -> 0; matrix products, arithmetic and copies ran while one was open for 7% -> 0% of each run, Pallas kernels for 0% -> 0%
where the time goes in v1:
time: 46.3 us; the launch traced here: 45.7 us
  Pallas kernels  36.9 us (80%)
  local copies, waits for them, and re-layouts  5.56 us (12%)
  other arithmetic  2.62 us (6%)
  between operations  0.64 us (1%)
    pallas_call x1, Pallas kernels, per_device(): pl.pallas_call(functools.partial(kernel, sizes), out_shape=(jax.ShapeDtyp...  36.9 us
    unnamed x3, local copies, waits for them, and re-layouts  5.56 us
    convert_element_type x1, other arithmetic, per_device(): sea.astype(f32)  1.31 us
    convert_element_type x1, other arithmetic, per_device(): count.astype(f32)  1.31 us

profile of v1, /device:TPU:0, one launch (start us, length us, event | category | flops | bytes accessed | tf_op | source)
XLA Modules:
  0.0 45.7 jit_solution(13909097848905743964)
XLA Ops:
  0.6 1.3 %convert_element_type.6.sea_ref = f32[24,128]{1,0:T(8,128)} convert(s32[24,128]{1,0:T(8,128)} %param.5) | non-fusion elementwise | flops 3072 | bytes 24576 | tf_op jit(solution)/shard_map/convert_element_type | solution.py:363
  1.9 1.3 %convert_element_type.7.count_ref = f32[24,128]{1,0:T(8,128)} convert(s32[24,128]{1,0:T(8,128)} %param.6) | non-fusion elementwise | flops 3072 | bytes 24576 | tf_op jit(solution)/shard_map/convert_element_type | solution.py:363
  3.2 36.9 %shard_map.67 = (f32[24,128]{1,0:T(8,128)}, f32[24,128]{1,0:T(8,128)}, f32[3840,128]{1,0:T(8,128)}) custom-call(f32[24,128]{1,0:T(8,128)} %forcing_ref.1, f32[24,128]{1,0:T(8,128)} %convert_element_type.6.sea_ref, f32[24,128]{1,0:T(8,128)} %convert_element_type.7.count_ref, f32[3840,128]{1,0:T(8,128)} %bitcast.2), custom_call_target="tpu_custom_call" | custom-call | tf_op jit(solution)/shard_map/pallas_call | solution.py:324
  40.2 1.3 %copy.10 = f32[24,128]{1,0:T(8,128)} copy(f32[24,128]{1,0:T(8,128)} %get-tuple-element.12) | data formatting | bytes 24576
  41.5 1.3 %copy.11 = f32[24,128]{1,0:T(8,128)} copy(f32[24,128]{1,0:T(8,128)} %get-tuple-element.13) | data formatting | bytes 24576
  42.8 2.9 %copy.12 = f32[4,40,24,128]{3,2,1,0:T(8,128)} copy(f32[4,40,24,128]{3,2,1,0:T(8,128)} %bitcast.3) | data formatting | bytes 3932160

commit v2 on v1

v2 whole, which is shorter than its diff:
```python
import functools

import jax
import jax.numpy as jnp
from jax import lax
from jax.experimental import pallas as pl
from jax.experimental.pallas import tpu as pltpu
from jax.sharding import PartitionSpec as P

ITERS = 4
DAMPING = 0.05
VISCOSITY = 0.02
STEP = 8
COLS = 4
MESH = pl.DeviceIdType.MESH


def east(a, b, lane):
    ra, rb = pltpu.roll(a, 127, 1), pltpu.roll(b, 127, 1)
    keep = lane < 127
    return jnp.where(keep, ra, rb), jnp.where(keep, rb, ra)


def west(a, b, lane):
    ra, rb = pltpu.roll(a, 1, 1), pltpu.roll(b, 1, 1)
    keep = lane > 0
    return jnp.where(keep, ra, rb), jnp.where(keep, rb, ra)


def north(x):
    return pltpu.roll(x, x.shape[0] - 1, 0)


def south(x):
    return pltpu.roll(x, 1, 0)


def kernel(
    sizes,
    forcing_ref, sea_ref, count_ref, state_ref,
    height_ref, resid_ref, tend_ref,
    q_ref, o_ref, side_ref, sidei_ref, vert_ref, verti_ref,
    rows_out, rows_in, cols_out, cols_in, corner_out, corner_in, strip_ref, slap_ref,
    face_ref, edge_ref, basis_ref, diag_ref, part_ref, lon_in, mid_ref, lat_in,
    load_sem, store_sem,
    side_sem, vert_sem, row_sem, col_sem, corner_sem, lon_sem, lat_sem,
):
    n_lon, n_lat, fields, levels, rows = sizes
    chunks = levels // STEP
    per_chunk = fields * STEP
    tall = rows + 8
    ilon, ilat = lax.axis_index("lon"), lax.axis_index("lat")
    has = {1: ilat < n_lat - 1, -1: ilat > 0}

    def at(dlon, dlat):
        return {
            "lon": lax.rem(ilon + dlon + n_lon, n_lon),
            "lat": lax.rem(ilat + dlat + n_lat, n_lat),
        }

    barrier = pltpu.get_barrier_semaphore()
    for off in range(1, n_lon):
        pl.semaphore_signal(barrier, inc=1, device_id=at(off, 0), device_id_type=MESH)
    for off in range(1, n_lat):
        pl.semaphore_signal(barrier, inc=1, device_id=at(0, off), device_id_type=MESH)
    for dlon, dlat in ((-1, -1), (1, -1), (-1, 1), (1, 1)):
        pl.semaphore_signal(barrier, inc=1, device_id=at(dlon, dlat), device_id_type=MESH)

    def span(c, f):
        return pl.ds((f * levels + c * STEP) * rows, STEP * rows)

    loads = []
    for c in range(chunks):
        loads.append([])
        for f in range(fields):
            load = pltpu.make_async_copy(
                state_ref.at[span(c, f)], q_ref.at[span(c, f)], load_sem.at[c, f]
            )
            load.start()
            loads[c].append(load)

    def remote(src, dst, sems, index, where):
        return pltpu.make_async_remote_copy(
            src_ref=src, dst_ref=dst, send_sem=sems.at[(0,) + index], recv_sem=sems.at[(1,) + index],
            device_id=where, device_id_type=MESH,
        )

    def send(*args):
        copy = remote(*args)
        copy.start()
        return copy

    def send_lat(copies, dlat):
        @pl.when(has[dlat])
        def _():
            for copy in copies:
                copy.start()

    def wait_lat(copies, dlat):
        @pl.when(has[dlat])
        def _():
            for copy in copies:
                copy.wait_send()

        @pl.when(has[-dlat])
        def _():
            for copy in copies:
                copy.wait_recv()

    for v, dlat in ((0, 1), (1, -1)):
        @pl.when(jnp.logical_not(has[dlat]))
        def _(v=v):
            vert_ref[v] = jnp.zeros_like(vert_ref[v])
            verti_ref[v] = jnp.zeros_like(verti_ref[v])
            corner_in[v] = jnp.zeros_like(corner_in[v])
            for c in range(chunks):
                rows_in[c, pl.ds(2 - 2 * v, 2)] = jnp.zeros_like(rows_in[c, pl.ds(2 - 2 * v, 2)])

    lane_r = lax.broadcasted_iota(jnp.int32, (rows, 128), 1)
    sub8 = lax.broadcasted_iota(jnp.int32, (8, 128), 0)
    lane8 = lax.broadcasted_iota(jnp.int32, (8, 128), 1)

    def pack(c):
        for load in loads[c]:
            load.wait()
        for i, j in enumerate((0, 1, rows - 2, rows - 1)):
            for f in range(fields):
                rows_out[c, i, pl.ds(f * STEP, STEP), :] = q_ref[
                    pl.ds((f * levels + c * STEP) * rows + j, STEP, stride=rows), :
                ]
        packed = jnp.zeros((rows, 128), jnp.float32)
        for f in range(fields):
            for kk in range(STEP):
                s = f * STEP + kk
                plane = q_ref[pl.ds((f * levels + c * STEP + kk) * rows, rows), :]
                moved = pltpu.roll(plane, (COLS * s + 2) % 128, 1)
                packed = jnp.where(lane_r // COLS == s, moved, packed)
        cols_out[c] = packed
        corner_out[c] = jnp.where(sub8 < 4, packed[:8], packed[rows - 8 :])

    pack(0)
    pl.semaphore_wait(barrier, n_lon + n_lat + 2)

    surface = ((forcing_ref, side_ref, vert_ref), (sea_ref, sidei_ref, verti_ref), (count_ref, sidei_ref, verti_ref))
    slot = (0, 0, 1)
    lon_blocks = []
    for i, (ref, side_in, _) in enumerate(surface):
        for side, dlon in ((0, 1), (1, -1)):
            lon_blocks.append(send(ref, side_in.at[slot[i], side], side_sem, (i, side), at(dlon, 0)))
    lat_blocks = []
    for v, dlat in ((0, -1), (1, 1)):
        part = pl.ds(0, 8) if v == 0 else pl.ds(rows - 8, 8)
        lat_blocks.append([
            remote(ref.at[part], vert_in.at[v, slot[i], h], vert_sem, (v, i, h), at(dlon, dlat))
            for i, (ref, _, vert_in) in enumerate(surface)
            for h, dlon in ((0, 1), (1, 0), (2, -1))
        ])
        send_lat(lat_blocks[v], dlat)

    col_copies, row_copies = [], []
    for c in range(chunks):
        if c > 0:
            pack(c)
        col_copies.append([
            send(cols_out.at[c], cols_in.at[c, h], col_sem, (c, h), at(dlon, 0))
            for h, dlon in ((0, 1), (1, -1))
        ])
        row_copies.append([])
        for v, dlat in ((0, -1), (1, 1)):
            row_copies[c].append(
                [remote(rows_out.at[c, pl.ds(2 * v, 2)], rows_in.at[c, pl.ds(2 - 2 * v, 2)],
                        row_sem, (c, v), at(0, dlat))]
                + [
                    remote(corner_out.at[c], corner_in.at[v, c, h], corner_sem, (c, v, h), at(dlon, dlat))
                    for h, dlon in ((0, 1), (1, -1))
                ]
            )
            send_lat(row_copies[c][v], dlat)

    for copy in lon_blocks:
        copy.wait()
    wait_lat(lat_blocks[0], -1)
    wait_lat(lat_blocks[1], 1)

    def torus(i):
        ref, side_in, vert_in = surface[i]
        j = slot[i]
        a = jnp.concatenate([ref[...], vert_in[0, j, 1], vert_in[1, j, 1]], axis=0)
        b = jnp.concatenate(
            [
                jnp.where(lane_r < 64, side_in[j, 1], side_in[j, 0]),
                jnp.where(lane8 < 64, vert_in[0, j, 2], vert_in[0, j, 0]),
                jnp.where(lane8 < 64, vert_in[1, j, 2], vert_in[1, j, 0]),
            ],
            axis=0,
        )
        return a.astype(jnp.float32), b.astype(jnp.float32)

    lane_t = lax.broadcasted_iota(jnp.int32, (rows + 16, 128), 1)
    force_a, force_b = torus(0)
    sea_a, sea_b = torus(1)
    count_a, count_b = torus(2)
    wet_a, wet_b = sea_a * count_a, sea_b * count_b
    depth_a, depth_b = wet_a / levels, wet_b / levels
    da, db = east(depth_a, depth_b, lane_t)
    ea, eb = jnp.minimum(depth_a, da), jnp.minimum(depth_b, db)
    wa, wb = west(ea, eb, lane_t)
    na, nb = jnp.minimum(depth_a, north(depth_a)), jnp.minimum(depth_b, north(depth_b))
    sa, sb = south(na), south(nb)
    diag_a = DAMPING + ea + wa + na + sa
    diag_b = DAMPING + eb + wb + nb + sb
    inv_a, inv_b = 1.0 / diag_a, 1.0 / diag_b
    va, vb = sea_a * force_a * inv_a, sea_b * force_b * inv_b
    ea, wa, na, sa = (c * inv_a for c in (ea, wa, na, sa))
    eb, wb, nb, sb = (c * inv_b for c in (eb, wb, nb, sb))
    diag = diag_a[:rows]
    diag_ref[...] = diag
    basis = [va[:rows]]
    for _ in range(ITERS):
        qe, qeb = east(va, vb, lane_t)
        qw, qwb = west(va, vb, lane_t)
        va, vb = (
            ea * qe + wa * qw + na * north(va) + sa * south(va),
            eb * qeb + wb * qwb + nb * north(vb) + sb * south(vb),
        )
        basis.append(va[:rows])
    for i, v in enumerate(basis):
        basis_ref[i] = v
    moments = []
    for m in range(2 * ITERS):
        moments.append(jnp.sum(diag * basis[m // 2] * basis[(m + 1) // 2], axis=0, keepdims=True))
    part_ref[...] = jnp.concatenate(moments, axis=0)
    lon_copies = [
        send(part_ref, lon_in.at[off - 1], lon_sem, (off - 1,), at(off, 0)) for off in range(1, n_lon)
    ]

    def squeeze(x):
        return jnp.concatenate([x[:rows], jnp.where(sub8 < 4, x[rows : rows + 8], x[rows + 8 :])], axis=0)

    wet_a, wet_b = squeeze(wet_a), squeeze(wet_b)
    lane = lax.broadcasted_iota(jnp.int32, (tall, 128), 1)
    wet_e, _ = east(wet_a, wet_b, lane)
    wet_w, _ = west(wet_a, wet_b, lane)
    for i, other in enumerate((wet_a, wet_e, wet_w, north(wet_a), south(wet_a))):
        face_ref[i] = jnp.minimum(wet_a, other)
    def spread(first, second):
        shape = (tall, 128)
        return jnp.where(lane % COLS < 2, jnp.broadcast_to(first, shape), jnp.broadcast_to(second, shape))

    wet_c = spread(wet_b[:, 0:1], wet_b[:, 127:128])
    wet_o = spread(wet_b[:, 1:2], wet_b[:, 126:127])
    wet_i = spread(wet_a[:, 127:128], wet_a[:, 0:1])
    for i, other in enumerate((wet_i, wet_o, north(wet_c), south(wet_c))):
        edge_ref[i] = jnp.minimum(wet_c, other)[:rows]

    near_r = lane_r % COLS < 2
    near = lane % COLS < 2

    def strips(c):
        for copy in col_copies[c]:
            copy.wait()
        wait_lat(row_copies[c][0], -1)
        wait_lat(row_copies[c][1], 1)
        outer = jnp.concatenate(
            [
                jnp.where(near_r, cols_in[c, 0], cols_in[c, 1]),
                jnp.where(
                    sub8 < 4,
                    jnp.where(lane8 % COLS < 2, corner_in[0, c, 0], corner_in[0, c, 1]),
                    jnp.where(lane8 % COLS < 2, corner_in[1, c, 0], corner_in[1, c, 1]),
                ),
            ],
            axis=0,
        )
        center = jnp.where(near, pltpu.roll(outer, 127, 1), pltpu.roll(outer, 1, 1))
        outer = jnp.where(near, pltpu.roll(outer, 126, 1), pltpu.roll(outer, 2, 1))[:rows]
        strip_ref[c] = center
        mid = center[:rows]
        kf = (c * STEP + (lane_r // COLS) % STEP).astype(jnp.float32)
        others = (cols_out[c], outer, north(center)[:rows], south(center)[:rows])
        total = jnp.zeros_like(mid)
        for i, other in enumerate(others):
            total = total + jnp.where(kf < edge_ref[i], other - mid, 0.0)
        slap_ref[c] = total

    def chunk(c):
        strips(c)

        def level(kk, carry):
            kf = (c * STEP + kk).astype(jnp.float32)
            here = kf < face_ref[0, pl.ds(0, rows), :]
            oe, ow, on, os = (kf < face_ref[i] for i in range(1, 5))
            oe_r, ow_r = oe[:rows], ow[:rows]

            def plane(f):
                s = f * STEP + kk
                base = pl.multiple_of((f * levels + c * STEP + kk) * rows, 8)
                one = pl.ds(s, 1)
                rim = jnp.where(
                    sub8 < 4,
                    jnp.where(sub8 == 0, rows_in[c, 2, one, :], rows_in[c, 3, one, :]),
                    jnp.where(sub8 == 6, rows_in[c, 0, one, :], rows_in[c, 1, one, :]),
                )
                q = jnp.concatenate([q_ref[pl.ds(base, rows), :], rim], axis=0)
                shift = lax.rem(254 - COLS * s, 128)
                edge = pltpu.roll(strip_ref[c], shift, 1)
                qe = jnp.where(lane < 127, pltpu.roll(q, 127, 1), edge)
                qw = jnp.where(lane > 0, pltpu.roll(q, 1, 1), edge)
                return base, shift, q, qe, qw, north(q), south(q)

            planes = {}
            planes[2] = plane(2)
            _, _, u, u_e, u_w, _, _ = planes[2]
            ue = jnp.where(oe_r, 0.25 * (u + u_e)[:rows], 0.0)
            uw = jnp.where(ow_r, 0.25 * (u + u_w)[:rows], 0.0)
            planes[3] = plane(3)
            _, _, v, _, _, v_n, v_s = planes[3]
            vn = jnp.where(on[:rows], 0.25 * (v + v_n)[:rows], 0.0)
            vs = jnp.where(os[:rows], 0.25 * (v + v_s)[:rows], 0.0)
            for f in (2, 3, 0, 1):
                base, shift, q, qe, qw, qn, qs = planes[f] if f in planes else plane(f)
                lap = (
                    jnp.where(oe, qe - q, 0.0) + jnp.where(ow, qw - q, 0.0)
                ) + (jnp.where(on, qn - q, 0.0) + jnp.where(os, qs - q, 0.0))
                near_lap = pltpu.roll(slap_ref[c], shift, 1)
                mid = lap[:rows]
                le = jnp.where(lane_r < 127, pltpu.roll(mid, 127, 1), near_lap)
                lw = jnp.where(lane_r > 0, pltpu.roll(mid, 1, 1), near_lap)
                ln, ls = north(lap)[:rows], south(lap)[:rows]
                again = (
                    jnp.where(oe_r, le - mid, 0.0) + jnp.where(ow_r, lw - mid, 0.0)
                ) + (jnp.where(on[:rows], ln - mid, 0.0) + jnp.where(os[:rows], ls - mid, 0.0))
                qm = q[:rows]
                flux = (ue * (qm + qe[:rows]) - uw * (qm + qw[:rows])) + (
                    vn * (qm + qn[:rows]) - vs * (qm + qs[:rows])
                )
                o_ref[pl.ds(base, rows), :] = jnp.where(here, -flux - VISCOSITY * again, 0.0)
            return carry

        lax.fori_loop(0, STEP, level, 0)
        stores = []
        for f in range(fields):
            store = pltpu.make_async_copy(
                o_ref.at[span(c, f)], tend_ref.at[span(c, f)], store_sem.at[c, f]
            )
            store.start()
            stores.append(store)
        return stores

    turn = min(2, chunks)
    stores = []
    for c in range(turn):
        stores += chunk(c)

    for copy in lon_copies:
        copy.wait()
    total = part_ref[...]
    for i in range(n_lon - 1):
        total = total + lon_in[i]
    mid_ref[...] = total
    lat_copies = [
        send(mid_ref, lat_in.at[off - 1], lat_sem, (off - 1,), at(0, off)) for off in range(1, n_lat)
    ]

    for c in range(turn, chunks):
        stores += chunk(c)

    for copy in lat_copies:
        copy.wait()
    total = mid_ref[...]
    for i in range(n_lat - 1):
        total = total + lat_in[i]
    total = jnp.broadcast_to(jnp.sum(total, axis=1, keepdims=True), (8, 128))
    mu = [total[m : m + 1] for m in range(2 * ITERS)]

    def inner(x, y):
        sums = [None] * (len(x) + len(y) - 1)
        for i, xi in enumerate(x):
            for j, yj in enumerate(y):
                sums[i + j] = xi * yj if sums[i + j] is None else sums[i + j] + xi * yj
        out = sums[0] * mu[0]
        for m in range(1, len(sums)):
            out = out + sums[m] * mu[m]
        return out

    one = jnp.ones((1, 128), jnp.float32)
    zero = jnp.zeros((1, 128), jnp.float32)
    z, p, h = [one], [one], []
    rz = mu[0]
    for it in range(ITERS):
        image = [hi - lo for hi, lo in zip(p + [zero], [zero] + p)]
        alpha = rz / inner(p, image)
        h = [x + alpha * y for x, y in zip(h + [zero], p)]
        z = [x - alpha * y for x, y in zip(z + [zero], image)]
        if it + 1 < ITERS:
            new = inner(z, z)
            beta = new / rz
            p = [x + beta * y for x, y in zip(z, p + [zero])]
            rz = new
    height = h[0] * basis_ref[0]
    for i in range(1, ITERS):
        height = height + h[i] * basis_ref[i]
    resid = z[0] * basis_ref[0]
    for i in range(1, ITERS + 1):
        resid = resid + z[i] * basis_ref[i]
    height_ref[...] = height
    resid_ref[...] = diag_ref[...] * resid
    for store in stores:
        store.wait()


def per_device(n_lon, n_lat, forcing, sea, count, state):
    fields, levels, rows, width = state.shape
    planes = fields * levels
    chunks = levels // STEP
    per_chunk = fields * STEP
    assert levels % STEP == 0 and per_chunk * COLS == width == 128 and rows % 8 == 0 and rows >= 16
    sizes = (n_lon, n_lat, fields, levels, rows)
    f32 = jnp.float32
    vmem = pl.BlockSpec(memory_space=pltpu.VMEM)
    hbm = pl.BlockSpec(memory_space=pl.ANY)
    dma = pltpu.SemaphoreType.DMA
    height, resid, tend = pl.pallas_call(
        functools.partial(kernel, sizes),
        out_shape=(
            jax.ShapeDtypeStruct((rows, width), f32),
            jax.ShapeDtypeStruct((rows, width), f32),
            jax.ShapeDtypeStruct((planes * rows, width), f32),
        ),
        in_specs=[vmem, vmem, vmem, hbm],
        out_specs=(vmem, vmem, hbm),
        scratch_shapes=[
            pltpu.VMEM((planes * rows, width), f32),
            pltpu.VMEM((planes * rows, width), f32),
            pltpu.VMEM((1, 2, rows, width), f32),
            pltpu.VMEM((2, 2, rows, width), jnp.int32),
            pltpu.VMEM((2, 1, 3, 8, width), f32),
            pltpu.VMEM((2, 2, 3, 8, width), jnp.int32),
            pltpu.VMEM((chunks, 4, per_chunk, width), f32),
            pltpu.VMEM((chunks, 4, per_chunk, width), f32),
            pltpu.VMEM((chunks, rows, width), f32),
            pltpu.VMEM((chunks, 2, rows, width), f32),
            pltpu.VMEM((chunks, 8, width), f32),
            pltpu.VMEM((2, chunks, 2, 8, width), f32),
            pltpu.VMEM((chunks, rows + 8, width), f32),
            pltpu.VMEM((chunks, rows, width), f32),
            pltpu.VMEM((5, rows + 8, width), f32),
            pltpu.VMEM((4, rows, width), f32),
            pltpu.VMEM((ITERS + 1, rows, width), f32),
            pltpu.VMEM((rows, width), f32),
            pltpu.VMEM((8, width), f32),
            pltpu.VMEM((n_lon - 1, 8, width), f32),
            pltpu.VMEM((8, width), f32),
            pltpu.VMEM((n_lat - 1, 8, width), f32),
            dma((chunks, fields)),
            dma((chunks, fields)),
            dma((2, 3, 2)),
            dma((2, 2, 3, 3)),
            dma((2, chunks, 2)),
            dma((2, chunks, 2)),
            dma((2, chunks, 2, 2)),
            dma((2, n_lon - 1)),
            dma((2, n_lat - 1)),
        ],
        compiler_params=pltpu.CompilerParams(collective_id=0, has_side_effects=True),
    )(forcing, sea, count, state.reshape(planes * rows, width))
    return height, resid, tend.reshape(state.shape)


def solution(mesh):
    return jax.shard_map(
        functools.partial(per_device, mesh.shape["lon"], mesh.shape["lat"]),
        mesh=mesh,
        in_specs=(P("lat", "lon"), P("lat", "lon"), P("lat", "lon"), P(None, None, "lat", "lon")),
        out_specs=(P("lat", "lon"), P("lat", "lon"), P(None, None, "lat", "lon")),
        check_vma=False,
    )
```

time: 46.3 us -> 28.9 us (0.62)
  Pallas kernels: 36.9 us -> 22.3 us
  other arithmetic: 2.62 us -> 0 us
    pallas_call x1, Pallas kernels: 36.9 us -> 22.3 us  [per_device(): pl.pallas_call(functools.partial(kernel, sizes), out_shape=(jax.ShapeDtyp...]
    convert_element_type x2 -> x0, other arithmetic: 2.62 us -> none  [the longest x1 1.31 us: per_device(): sea.astype(f32)]
where the time goes in v2:
time: 28.9 us; the launch traced here: 28.5 us
  Pallas kernels  22.3 us (77%)
  local copies, waits for them, and re-layouts  5.56 us (19%)
  between operations  0.64 us (2%)
    pallas_call x1, Pallas kernels, per_device(): pl.pallas_call(functools.partial(kernel, sizes), out_shape=(jax.ShapeDtyp...  22.3 us
    unnamed x3, local copies, waits for them, and re-layouts  5.56 us

profile of v2, /device:TPU:0, one launch (start us, length us, event | category | flops | bytes accessed | tf_op | source)
XLA Modules:
  0.0 28.5 jit_solution(10565146650493543719)
XLA Ops:
  0.6 22.3 %shard_map.67 = (f32[24,128]{1,0:T(8,128)}, f32[24,128]{1,0:T(8,128)}, f32[3840,128]{1,0:T(8,128)}) custom-call(f32[24,128]{1,0:T(8,128)} %forcing_ref.1, s32[24,128]{1,0:T(8,128)} %sea_ref.1, s32[24,128]{1,0:T(8,128)} %count_ref.1, f32[3840,128]{1,0:T(8,128)} %bitcast.2), custom_call_target="tpu_custom_call" | custom-call | tf_op jit(solution)/shard_map/pallas_call | solution.py:423
  22.9 1.3 %copy.10 = f32[24,128]{1,0:T(8,128)} copy(f32[24,128]{1,0:T(8,128)} %get-tuple-element.12) | data formatting | bytes 24576
  24.2 1.3 %copy.11 = f32[24,128]{1,0:T(8,128)} copy(f32[24,128]{1,0:T(8,128)} %get-tuple-element.13) | data formatting | bytes 24576
  25.5 2.9 %copy.12 = f32[4,40,24,128]{3,2,1,0:T(8,128)} copy(f32[4,40,24,128]{3,2,1,0:T(8,128)} %bitcast.3) | data formatting | bytes 3932160

commit v3 on v2

--- a/solution.py
+++ b/solution.py
@@ -405,6 +405,23 @@
         resid = resid + z[i] * basis_ref[i]
     height_ref[...] = height
     resid_ref[...] = diag_ref[...] * resid
+    for store in stores:
+        store.wait()
+
+
+def deliver(height_in, resid_in, tend_in, height_ref, resid_ref, tend_ref, h_buf, r_buf, t_buf, in_sem, out_sem):
+    pieces = in_sem.shape[0] - 2
+    size = t_buf.shape[0] // pieces
+    moves = [(tend_in.at[pl.ds(i * size, size)], t_buf.at[pl.ds(i * size, size)], tend_ref.at[pl.ds(i * size, size)])
+             for i in range(pieces)]
+    moves += [(height_in, h_buf, height_ref), (resid_in, r_buf, resid_ref)]
+    loads = [pltpu.make_async_copy(src, buf, in_sem.at[i]) for i, (src, buf, _) in enumerate(moves)]
+    stores = [pltpu.make_async_copy(buf, dst, out_sem.at[i]) for i, (_, buf, dst) in enumerate(moves)]
+    for load in loads:
+        load.start()
+    for load, store in zip(loads, stores):
+        load.wait()
+        store.start()
     for store in stores:
         store.wait()
 
@@ -464,6 +481,21 @@
         ],
         compiler_params=pltpu.CompilerParams(collective_id=0, has_side_effects=True),
     )(forcing, sea, count, state.reshape(planes * rows, width))
+    small = jax.ShapeDtypeStruct((rows, width), f32)
+    pieces = 2 * fields
+    height, resid, tend = pl.pallas_call(
+        deliver,
+        out_shape=(small, small, jax.ShapeDtypeStruct((planes * rows, width), f32)),
+        in_specs=[hbm] * 3,
+        out_specs=(hbm,) * 3,
+        scratch_shapes=[
+            pltpu.VMEM((rows, width), f32),
+            pltpu.VMEM((rows, width), f32),
+            pltpu.VMEM((planes * rows, width), f32),
+            dma((pieces + 2,)),
+            dma((pieces + 2,)),
+        ],
+    )(height, resid, tend)
     return height, resid, tend.reshape(state.shape)
 
 

time: 28.9 us -> 25.7 us (0.89)
  local copies, waits for them, and re-layouts: 5.56 us -> 0 us
  Pallas kernels: 22.3 us -> 24.8 us
    unnamed x3 -> x0, local copies, waits for them, and re-layouts: 5.56 us -> none
    pallas_call x0 -> x1, Pallas kernels: none -> 2.51 us  [per_device(): pl.pallas_call(deliver, out_shape=(small, small, jax.ShapeDtypeStruct((pl...]
where the time goes in v3:
time: 25.7 us; the launch traced here: 25.4 us
  Pallas kernels  24.8 us (96%)
  between operations  0.64 us (2%)
    pallas_call x1, Pallas kernels, per_device(): pl.pallas_call(functools.partial(kernel, sizes), out_shape=(jax.ShapeDtyp...  22.3 us
    pallas_call x1, Pallas kernels, per_device(): pl.pallas_call(deliver, out_shape=(small, small, jax.ShapeDtypeStruct((pl...  2.51 us

profile of v3, /device:TPU:0, one launch (start us, length us, event | category | flops | bytes accessed | tf_op | source)
XLA Modules:
  0.0 25.4 jit_solution(10151634324012104727)
XLA Ops:
  0.6 22.3 %shard_map.67 = (f32[24,128]{1,0:T(8,128)}, f32[24,128]{1,0:T(8,128)}, f32[3840,128]{1,0:T(8,128)}) custom-call(f32[24,128]{1,0:T(8,128)} %forcing_ref.1, s32[24,128]{1,0:T(8,128)} %sea_ref.1, s32[24,128]{1,0:T(8,128)} %count_ref.1, f32[3840,128]{1,0:T(8,128)} %bitcast.2), custom_call_target="tpu_custom_call" | custom-call | tf_op jit(solution)/shard_map/pallas_call | solution.py:440
  22.9 2.5 %shard_map.68 = (f32[24,128]{1,0:T(8,128)}, f32[24,128]{1,0:T(8,128)}, f32[3840,128]{1,0:T(8,128)}) custom-call(f32[24,128]{1,0:T(8,128)} %get-tuple-element.9.height_in, f32[24,128]{1,0:T(8,128)} %get-tuple-element.10.resid_in, f32[3840,128]{1,0:T(8,128)} %get-tuple-element.11.tend_in), custom_call_target="tpu_custom_call" | custom-call | tf_op jit(solution)/shard_map/pallas_call | solution.py:486
